TPU v7x, 128 devices: a whole 4x4x4 slice. The times are simulated.
128 devices in a mesh: dp: 1, tp2: 64 (over z, y, x), tp: 2 (over core).
Axes of the slice: x: 4, y: 4, z: 4, core: 2. Of those that a mesh axis runs over, the one named last changes fastest.
Arguments:
- attn_out: bfloat16 [8192, 8192], P('dp', 'tp')
- w_out: bfloat16 [8192, 8192], P('tp', 'tp2')
- residual: bfloat16 [8192, 8192], P(('dp', 'tp'), 'tp2')
- norm_gain: float32 [8192], P('tp2')
Outputs:
- output 1: bfloat16 [8192, 8192], P(('dp', 'tp'), 'tp2')
- output 2: bfloat16 [8192, 8192], P(('dp', 'tp'), 'tp2')
All inputs are finite; a program needn't handle non-finite values.
Results may differ from a plain program's by a relative error of at most 0.00667563.
Values are sent between devices in bfloat16 or wider.
A program may use at most 1 GiB of HBM per device.

v0:
```python
import jax
import jax.numpy as jnp
from jax import lax
from jax.sharding import PartitionSpec as P, NamedSharding

EPS_NORM = 1e-6


def solution(mesh):
    tp_size = mesh.shape["tp"]
    col_groups = mesh.shape["tp2"]

    def local_step(attn_blk, w_blk, res_blk, gain_blk):
        block_prod = jnp.dot(attn_blk, w_blk, preferred_element_type=jnp.float32).astype(jnp.bfloat16)
        token_rows, local_cols = block_prod.shape
        received = lax.all_to_all(block_prod, "tp", 0, 0, tiled=True)
        y_sum = jnp.sum(received.reshape(tp_size, token_rows // tp_size, local_cols), axis=0, dtype=jnp.float32)
        hidden = res_blk.astype(jnp.float32) + y_sum
        sq_sum = lax.psum(jnp.sum(hidden * hidden, axis=-1, keepdims=True), "tp2")
        inv_rms = lax.rsqrt(sq_sum / (local_cols * col_groups) + EPS_NORM)
        normed = hidden * inv_rms * gain_blk
        return hidden.astype(jnp.bfloat16), normed.astype(jnp.bfloat16)

    row_spec = P(("dp", "tp"), "tp2")
    return jax.shard_map(local_step, mesh=mesh, in_specs=(P("dp", "tp"), P("tp", "tp2"), row_spec, P("tp2")), out_specs=(row_spec, row_spec), check_vma=False)
```

profile of v0, /device:TPU:0, one launch (start us, length us, event | category | flops | bytes accessed | tf_op | source)
XLA Modules:
  0.0 388.0 jit_solution(17456503022265444922)
XLA Ops:
  0.6 0.0 copy-start
  0.6 1.2 copy-done
  1.9 25.8 %convolution_convert_fusion = bf16[8192,128]{1,0:T(8,128)(2,1)S(1)} fusion(bf16[8192,4096]{1,0:T(8,128)(2,1)} %param.4, bf16[4096,128]{1,0:T(8,128)(2,1)S(1)} %copy-done), kind=kOutput, calls=%fused_computation | convolution fusion | flops 8590983168 | bytes 70254592 | tf_op jit(solution)/shard_map/dot_general | solution.py:14
  27.7 5.4 %all_to_all.9 = bf16[2,4096,128]{2,1,0:T(8,128)(2,1)S(1)} all-to-all(bf16[2,4096,128]{2,1,0:T(8,128)(2,1)S(1)} %bitcast.5), channel_id=1, replica_groups=mesh['dp'=1,'tp2'=64,'tp'=2] {'tp'}, dimensions={0} | all-to-all | bytes 4194304 | tf_op jit(solution)/shard_map/all_to_all | solution.py:16
  33.1 0.0 copy-start.1
  33.1 0.4 convert_reduce_fusion
  33.5 0.9 copy-done.1
  34.4 0.0 copy-start.2
  34.4 0.7 multiply_reduce_fusion
  35.0 350.3 %psum.7 = f32[4096,1]{0,1:T(1,128)S(1)} all-reduce(f32[4096,1]{0,1:T(1,128)S(1)} %bitcast.7), channel_id=1, replica_groups=mesh['dp'=1,'tp2'=64,'tp'=2] {'tp2'}, use_global_device_ids=true, to_apply=%region_2.0 | all-reduce | flops 4096 | bytes 32768 | tf_op jit(solution)/shard_map/psum | solution.py:19
  385.3 0.0 copy-done.2
  385.3 2.7 multiply_convert_fusion
  (1 shorter events, 0.0 us)
Async XLA Ops:
  0.6 1.2 copy-start
  33.1 1.2 copy-start.1
  34.4 351.0 %copy-start.2 = (f32[128]{0:T(128)S(1)}, f32[128]{0:T(128)}, u32[]{:S(2)}) copy-start(f32[128]{0:T(128)} %param.7) | copy-start | bytes 1540
where the time goes:
time: 388 us
  blocking collectives  356 us (92%)
  matrix products  25.8 us (7%)
    psum x1, blocking collectives, local_step(): sq_sum = lax.psum(jnp.sum(hidden * hidden, axis=-1, keepdims=True), 'tp2')  350 us
    dot_general x1, matrix products, local_step(): jnp.dot(attn_blk, w_blk, preferred_element_type=jnp.float32)  25.8 us

commit v1 on v0

v1 whole, which is shorter than its diff:
```python
import functools
import itertools

import jax
import jax.numpy as jnp
from jax import lax
from jax.experimental import pallas as pl
from jax.experimental.pallas import tpu as pltpu
from jax.sharding import PartitionSpec as P

EPS_NORM = 1e-6
MESH = pl.DeviceIdType.MESH
F32, BF16 = jnp.float32, jnp.bfloat16

T = 256
NB = 6
AHEAD = 4
HEAD = 2
BARRIER_AT = 5
EPI_FROM = 8
GROUPS = 4
SIDE = 4


def ring_distance(d):
    return min(d, SIDE - d)


OFFSETS = sorted(
    (o for o in itertools.product(range(SIDE), repeat=3) if any(o)),
    key=lambda o: -sum(map(ring_distance, o)),
)
PEERS = len(OFFSETS)


def kernel(a, w, res, gain, h_out, n_out, abuf, wbuf, rbuf, gbuf, sendbuf, recvbuf, ybuf, hbuf, sq, parts,
           a_sem, w_sem, r_sem, g_sem, psend_sem, precv_sem, qsend_sem, qrecv_sem):
    core = lax.axis_index("tp")
    me = lax.axis_index("tp2")
    z, y, x = me // (SIDE * SIDE), (me // SIDE) % SIDE, me % SIDE
    own_rows = h_out.shape[0]
    n = own_rows // T
    width = w.shape[1] * (PEERS + 1)
    rows128 = own_rows // 128 // GROUPS
    chunks = n // GROUPS

    def peer(o):
        return {"tp2": ((z + o[0]) % SIDE) * (SIDE * SIDE) + ((y + o[1]) % SIDE) * SIDE + (x + o[2]) % SIDE}

    partner = {"tp": 1 - core}

    def chunk_row(q):
        if isinstance(q, int):
            mine, j = (False, 0) if q == 0 else (True, n - 1) if q == 2 * n - 1 else (q % 2 == 0, (q - 1) // 2 + (q % 2))
            half = core if mine else 1 - core
        else:
            first, last, even = q == 0, q == 2 * n - 1, q % 2 == 0
            mine = jnp.logical_and(jnp.logical_or(even, last), jnp.logical_not(first))
            j = jnp.where(first, 0, jnp.where(last, n - 1, (q - 1) // 2 + q % 2))
            half = jnp.where(mine, core, 1 - core)
        return pl.multiple_of(half * own_rows + j * T, T)

    def a_copy(q):
        slot = q % NB
        return pltpu.make_async_copy(a.at[pl.ds(chunk_row(q), T)], abuf.at[slot], a_sem.at[slot])

    w_copy = pltpu.make_async_copy(w, wbuf, w_sem)
    r_copy = pltpu.make_async_copy(res, rbuf, r_sem)
    g_copy = pltpu.make_async_copy(gain, gbuf, g_sem)

    w_copy.start()
    for q in range(HEAD):
        a_copy(q).start()

    barrier = pltpu.get_barrier_semaphore()
    for o in OFFSETS:
        pl.semaphore_signal(barrier, inc=1, device_id=peer(o), device_id_type=MESH)
    pl.semaphore_signal(barrier, inc=1, device_id=partner, device_id_type=MESH)

    def rows_of(j):
        return pl.ds(pl.multiple_of(j * T, T), T)

    def partner_copy(first, count):
        rows = pl.ds(pl.multiple_of(first * T, T), count * T)
        return pltpu.make_async_remote_copy(
            src_ref=sendbuf.at[rows], dst_ref=recvbuf.at[rows], send_sem=psend_sem.at[first], recv_sem=precv_sem.at[first],
            device_id=partner, device_id_type=MESH,
        )

    def finish_h(e, group):
        rows = rows_of(e)
        total = ybuf[rows, :].astype(F32) + recvbuf[rows, :].astype(F32)
        h = rbuf[rows, :].astype(F32) + total
        hbuf[rows, :] = h
        h_out[rows, :] = h.astype(BF16)
        squares = h * h
        for b in range(T // 128):
            block = jnp.transpose(squares[b * 128:(b + 1) * 128, :])
            sq[group, pl.ds((e % chunks) * (T // 128) + b, 1), :] = jnp.sum(block, axis=0, keepdims=True)

    def send_squares(group):
        parts[group, me] = sq[group]
        for o in OFFSETS:
            pltpu.make_async_remote_copy(
                src_ref=sq.at[group], dst_ref=parts.at[group, me], send_sem=qsend_sem.at[group],
                recv_sem=qrecv_sem.at[group], device_id=peer(o), device_id_type=MESH,
            ).start()

    def wait_squares(group, sem):
        pltpu.make_async_copy(parts.at[group, pl.ds(0, PEERS)], parts.at[group, pl.ds(0, PEERS)], sem.at[group]).wait()

    def finish_n(group):
        wait_squares(group, qrecv_sem)
        inv = lax.rsqrt(jnp.sum(parts[group], axis=0) / width + EPS_NORM)
        g = gbuf[...]
        for i in range(rows128):
            rows = pl.ds((group * rows128 + i) * 128, 128)
            scale = jnp.transpose(jnp.broadcast_to(inv[i:i + 1, :], (128, 128)))
            n_out[rows, :] = (hbuf[rows, :] * scale * g).astype(BF16)

    def main():
        def product(q):
            slot = q % NB
            a_copy(q).wait()
            return slot

        def take(slot):
            return jnp.dot(abuf[slot], wbuf[...], preferred_element_type=F32).astype(BF16)

        def request(q):
            if isinstance(q, int):
                if q < 2 * n:
                    a_copy(q).start()
            else:
                @pl.when(q < 2 * n)
                def _():
                    a_copy(q).start()

        w_copy.wait()
        for q in range(HEAD, AHEAD + 1):
            request(q)
        slot = product(0)
        sendbuf[rows_of(0), :] = take(slot)
        r_copy.start()
        g_copy.start()

        def step(j, extra):
            request(2 * j + AHEAD + 1)
            request(2 * j + AHEAD + 2)
            theirs = product(2 * j + 1)
            mine = product(2 * j + 2)
            sendbuf[rows_of(j + 1), :] = take(theirs)
            ybuf[rows_of(j), :] = take(mine)
            extra()

        def loop(low, high, extra=lambda j: None, after=lambda j: None):
            def body(j, _):
                step(j, lambda: extra(j))
                after(j)
                return 0

            lax.fori_loop(low, high, body, 0)

        loop(0, BARRIER_AT + 1)
        pl.semaphore_wait(barrier, PEERS + 1)
        first = BARRIER_AT + 2
        partner_copy(0, first).start()

        def send(j):
            partner_copy(j + 1, 1).start()

        loop(BARRIER_AT + 1, EPI_FROM, after=send)
        partner_copy(0, first).wait_recv()
        r_copy.wait()
        g_copy.wait()

        e = 0
        j = EPI_FROM
        while j < n - 1:
            group = e // chunks
            steps = min(chunks // 2, n - 1 - j)

            def extra(jj, base=e - 2 * j, group=group):
                for b in range(2):
                    e_now = base + 2 * jj + b
                    if True:
                        finish_h(e_now, group)

            if e >= first or e + 2 * steps > first:
                inner = extra

                def extra(jj, inner=inner, base=e - 2 * j):
                    for b in range(2):
                        e_now = base + 2 * jj + b

                        @pl.when(e_now >= first)
                        def _():
                            partner_copy(e_now, 1).wait_recv()

                    inner(jj)

            loop(j, j + steps, extra=extra, after=send)
            j += steps
            e += 2 * steps
            if e % chunks == 0:
                send_squares(e // chunks - 1)

        slot = product(2 * n - 1)
        ybuf[rows_of(n - 1), :] = take(slot)
        while e < n - 1:
            partner_copy(e, 1).wait_recv()
            finish_h(e, e // chunks)
            e += 1
        partner_copy(n - 1, 1).wait_recv()
        finish_h(n - 1, GROUPS - 1)
        send_squares(GROUPS - 1)
        for group in range(GROUPS):
            finish_n(group)
        partner_copy(0, first).wait_send()
        for j in range(first, n):
            partner_copy(j, 1).wait_send()
        for group in range(GROUPS):
            wait_squares(group, qsend_sem)

    main()


def solution(mesh):
    def local_step(attn_blk, w_blk, res_blk, gain_blk):
        rows, cols = res_blk.shape
        n = rows // T
        rows128 = rows // 128 // GROUPS
        hbm = pl.BlockSpec(memory_space=pltpu.HBM)
        vmem = pl.BlockSpec(memory_space=pltpu.VMEM)
        out = jax.ShapeDtypeStruct((rows, cols), BF16)
        return pl.pallas_call(
            kernel,
            out_shape=(out, out),
            in_specs=[hbm] * 4,
            out_specs=(vmem, vmem),
            scratch_shapes=[
                pltpu.VMEM((NB, T, attn_blk.shape[1]), BF16),
                pltpu.VMEM(w_blk.shape, BF16),
                pltpu.VMEM((rows, cols), BF16),
                pltpu.VMEM((1, cols), F32),
                pltpu.VMEM((rows, cols), BF16),
                pltpu.VMEM((rows, cols), BF16),
                pltpu.VMEM((rows, cols), BF16),
                pltpu.VMEM((rows, cols), F32),
                pltpu.VMEM((GROUPS, rows128, 128), F32),
                pltpu.VMEM((GROUPS, PEERS + 1, rows128, 128), F32),
                pltpu.SemaphoreType.DMA((NB,)),
                pltpu.SemaphoreType.DMA,
                pltpu.SemaphoreType.DMA,
                pltpu.SemaphoreType.DMA,
                pltpu.SemaphoreType.DMA((n,)),
                pltpu.SemaphoreType.DMA((n,)),
                pltpu.SemaphoreType.DMA((GROUPS,)),
                pltpu.SemaphoreType.DMA((GROUPS,)),
            ],
            compiler_params=pltpu.CompilerParams(collective_id=0, has_side_effects=True, vmem_limit_bytes=40 * 2**20),
        )(*(pltpu.with_memory_space_constraint(v, pltpu.HBM) for v in (attn_blk, w_blk, res_blk, gain_blk.reshape(1, cols))))

    row_spec = P(("dp", "tp"), "tp2")
    return jax.shard_map(
        local_step, mesh=mesh, in_specs=(P("dp", "tp"), P("tp", "tp2"), row_spec, P("tp2")),
        out_specs=(row_spec, row_spec), check_vma=False,
    )
```

time: 388 us -> 41 us (0.11)
  blocking collectives: 356 us -> 0 us
  Pallas kernels: 0 us -> 38.3 us
  matrix products: 25.8 us -> 0 us
    psum x1 -> x0, blocking collectives: 350 us -> none  [local_step(): sq_sum = lax.psum(jnp.sum(hidden * hidden, axis=-1, keepdims=True), 'tp2')]
    pallas_call x0 -> x1, Pallas kernels: none -> 38.3 us  [local_step(): pl.pallas_call(kernel, out_shape=(out, out), in_specs=[hbm] * 4, out_spec...]
    dot_general x1 -> x0, matrix products: 25.8 us -> none  [local_step(): jnp.dot(attn_blk, w_blk, preferred_element_type=jnp.float32)]
    all_to_all x1 -> x0, blocking collectives: 5.43 us -> none  [local_step(): received = lax.all_to_all(block_prod, 'tp', 0, 0, tiled=True)]
where the time goes in v1:
time: 41 us; the launch traced here: 40.9 us
  Pallas kernels  38.3 us (93%)
  local copies, waits for them, and re-layouts  1.94 us (5%)
  between operations  0.64 us (2%)
    pallas_call x1, Pallas kernels, local_step(): pl.pallas_call(kernel, out_shape=(out, out), in_specs=[hbm] * 4, out_spec...  38.3 us
    unnamed x2, local copies, waits for them, and re-layouts  1.94 us

profile of v1, /device:TPU:0, one launch (start us, length us, event | category | flops | bytes accessed | tf_op | source)
XLA Modules:
  0.0 40.9 jit_solution(7884242566539712954)
XLA Ops:
  0.6 38.3 %shard_map.59 = (bf16[4096,128]{1,0:T(8,128)(2,1)S(1)}, bf16[4096,128]{1,0:T(8,128)(2,1)S(1)}) custom-call(bf16[8192,4096]{1,0:T(8,128)(2,1)} %a.1, bf16[4096,128]{1,0:T(8,128)(2,1)} %w.1, bf16[4096,128]{1,0:T(8,128)(2,1)} %res.1, f32[1,128]{1,0:T(1,128)} %bitcast.1), custom_call_target="tpu_custom_call" | custom-call | tf_op jit(solution)/shard_map/pallas_call | solution.py:236
  38.9 1.0 %copy.8 = bf16[4096,128]{1,0:T(8,128)(2,1)} copy(bf16[4096,128]{1,0:T(8,128)(2,1)S(1)} %get-tuple-element.4) | data formatting | bytes 2097152
  39.9 1.0 %copy.9 = bf16[4096,128]{1,0:T(8,128)(2,1)} copy(bf16[4096,128]{1,0:T(8,128)(2,1)S(1)} %get-tuple-element.5) | data formatting | bytes 2097152

commit v2 on v1

v2 whole, which is shorter than its diff:
```python
import itertools

import jax
import jax.numpy as jnp
from jax import lax
from jax.experimental import pallas as pl
from jax.experimental.pallas import tpu as pltpu
from jax.sharding import PartitionSpec as P

EPS_NORM = 1e-6
MESH = pl.DeviceIdType.MESH
F32, BF16 = jnp.float32, jnp.bfloat16

T = 256
NB = 8
AHEAD = 6
HEAD = 2
BARRIER_AT = 4
EPI_FROM = 7
STAGED = (8, 5)
SIDE = 4
OUT_PARTS = 2


def ring_distance(d):
    return min(d, SIDE - d)


OFFSETS = sorted(
    (o for o in itertools.product(range(SIDE), repeat=3) if any(o)),
    key=lambda o: -sum(map(ring_distance, o)),
)
PEERS = len(OFFSETS)
STAGES = tuple(tuple(tuple(d if i == axis else 0 for i in range(3)) for d in (2, 1, 3)) for axis in (2, 1, 0))


def kernel(a, w, res, gain, h_out, n_out, abuf, wbuf, rbuf, gbuf, sendbuf, recvbuf, ybuf, hbuf, last_sq, last_parts, *rest):
    n_staged = len(STAGED)
    staged_sq, staged_parts, rest = rest[:n_staged], rest[n_staged:2 * n_staged], rest[2 * n_staged:]
    a_sem, w_sem, r_sem, g_sem, psend_sem, precv_sem, qsend_sem, qrecv_sem, ssend_sem, srecv_sem = rest
    core = lax.axis_index("tp")
    me = lax.axis_index("tp2")
    z, y, x = me // (SIDE * SIDE), (me // SIDE) % SIDE, me % SIDE
    own_rows = h_out.shape[0]
    n = own_rows // T
    per = T // 128
    width = w.shape[1] * (PEERS + 1)

    def peer(o):
        return {"tp2": ((z + o[0]) % SIDE) * (SIDE * SIDE) + ((y + o[1]) % SIDE) * SIDE + (x + o[2]) % SIDE}

    partner = {"tp": 1 - core}

    def chunk_row(q):
        if isinstance(q, int):
            mine, j = (False, 0) if q == 0 else (True, n - 1) if q == 2 * n - 1 else (q % 2 == 0, (q - 1) // 2 + (q % 2))
            half = core if mine else 1 - core
        else:
            first, last, even = q == 0, q == 2 * n - 1, q % 2 == 0
            mine = jnp.logical_and(jnp.logical_or(even, last), jnp.logical_not(first))
            j = jnp.where(first, 0, jnp.where(last, n - 1, (q - 1) // 2 + q % 2))
            half = jnp.where(mine, core, 1 - core)
        return pl.multiple_of(half * own_rows + j * T, T)

    def a_copy(q):
        slot = q % NB
        return pltpu.make_async_copy(a.at[pl.ds(chunk_row(q), T)], abuf.at[slot], a_sem.at[slot])

    w_copy = pltpu.make_async_copy(w, wbuf, w_sem)
    r_copy = pltpu.make_async_copy(res, rbuf, r_sem)
    g_copy = pltpu.make_async_copy(gain, gbuf, g_sem)

    w_copy.start()
    for q in range(HEAD):
        a_copy(q).start()

    barrier = pltpu.get_barrier_semaphore()
    for o in OFFSETS:
        pl.semaphore_signal(barrier, inc=1, device_id=peer(o), device_id_type=MESH)
    pl.semaphore_signal(barrier, inc=1, device_id=partner, device_id_type=MESH)

    def rows_of(j):
        return pl.ds(pl.multiple_of(j * T, T), T)

    def partner_copy(first, count):
        rows = pl.ds(pl.multiple_of(first * T, T), count * T)
        return pltpu.make_async_remote_copy(
            src_ref=sendbuf.at[rows], dst_ref=recvbuf.at[rows], send_sem=psend_sem.at[first], recv_sem=precv_sem.at[first],
            device_id=partner, device_id_type=MESH,
        )

    def finish_h(e, sums, at):
        rows = rows_of(e)
        total = ybuf[rows, :].astype(F32) + recvbuf[rows, :].astype(F32)
        h = rbuf[rows, :].astype(F32) + total
        hbuf[rows, :] = h
        h_out[rows, :] = h.astype(BF16)
        squares = h * h
        for b in range(per):
            block = jnp.transpose(squares[b * 128:(b + 1) * 128, :])
            sums[pl.ds(at * per + b, 1), :] = jnp.sum(block, axis=0, keepdims=True)

    def send_stage(group, stage):
        parts = staged_parts[group]
        here = (x, y, z)[stage]
        parts[stage, here] = staged_sq[group][stage]
        for o in STAGES[stage]:
            pltpu.make_async_remote_copy(
                src_ref=staged_sq[group].at[stage], dst_ref=parts.at[stage, here], send_sem=ssend_sem.at[group, stage],
                recv_sem=srecv_sem.at[group, stage], device_id=peer(o), device_id_type=MESH,
            ).start()

    def wait_stage(group, stage, sem):
        whole = staged_parts[group].at[stage, pl.ds(0, SIDE - 1)]
        pltpu.make_async_copy(whole, whole, sem.at[group, stage]).wait()

    def next_stage(group, stage):
        wait_stage(group, stage - 1, srecv_sem)
        staged_sq[group][stage] = jnp.sum(staged_parts[group][stage - 1], axis=0)
        send_stage(group, stage)

    def staged_sums(group):
        wait_stage(group, len(STAGES) - 1, srecv_sem)
        return jnp.sum(staged_parts[group][len(STAGES) - 1], axis=0)

    def send_last():
        for o in OFFSETS:
            pltpu.make_async_remote_copy(
                src_ref=last_sq, dst_ref=last_parts.at[me], send_sem=qsend_sem, recv_sem=qrecv_sem,
                device_id=peer(o), device_id_type=MESH,
            ).start()
        last_parts[me] = last_sq[...]

    def wait_last(sem):
        whole = last_parts.at[pl.ds(0, PEERS)]
        pltpu.make_async_copy(whole, whole, sem).wait()

    def finish_n(first, sums):
        inv = lax.rsqrt(sums / width + EPS_NORM)
        g = gbuf[...]
        for i in range(sums.shape[0]):
            rows = pl.ds(first * T + i * 128, 128)
            scale = jnp.transpose(jnp.broadcast_to(inv[i:i + 1, :], (128, 128)))
            n_out[rows, :] = (hbuf[rows, :] * scale * g).astype(BF16)

    def request(q):
        if isinstance(q, int):
            if q < 2 * n:
                a_copy(q).start()
        else:
            @pl.when(q < 2 * n)
            def _():
                a_copy(q).start()

    def product(q):
        return jnp.dot(abuf[q % NB], wbuf[...], preferred_element_type=F32).astype(BF16)

    def loop(low, high, before=lambda j: None, after=lambda j: None):
        def body(j, _):
            request(2 * j + AHEAD + 1)
            request(2 * j + AHEAD + 2)
            a_copy(2 * j + 1).wait()
            a_copy(2 * j + 2).wait()
            before(j)
            sendbuf[rows_of(j + 1), :] = product(2 * j + 1)
            ybuf[rows_of(j), :] = product(2 * j + 2)
            after(j)
            return 0

        lax.fori_loop(low, high, body, 0)

    w_copy.wait()
    for q in range(HEAD, AHEAD + 1):
        request(q)
    a_copy(0).wait()
    sendbuf[rows_of(0), :] = product(0)
    r_copy.start()
    g_copy.start()
    loop(0, BARRIER_AT + 1)

    pl.semaphore_wait(barrier, PEERS + 1)
    first = BARRIER_AT + 2
    partner_copy(0, first).start()

    def send(j):
        partner_copy(j + 1, 1).start()

    loop(BARRIER_AT + 1, EPI_FROM, after=send)
    partner_copy(0, first).wait_recv()
    r_copy.wait()
    g_copy.wait()

    ends = [sum(STAGED[:i + 1]) for i in range(n_staged)]

    def place(e):
        for group, end in enumerate(ends):
            if e < end:
                return staged_sq[group].at[0], end - STAGED[group]
        return last_sq, ends[-1]

    def events(done):
        for group, end in enumerate(ends):
            if done == end:
                send_stage(group, 0)

    e, j = 0, EPI_FROM
    stage_of = [None] * n_staged
    while j < n - 1:
        count = 2 if e + 2 <= j else 1
        sums, base = place(e)
        steps = 1
        while (
            j + steps < n - 1 and (2 if e + count * steps + 2 <= j + steps else 1) == count
            and place(e + count * steps)[1] == base and e + count * steps not in ends
            and (e >= first) == (e + count * steps >= first)
        ):
            steps += 1

        def before(jj, e=e, j=j, count=count, sums=sums, base=base):
            for b in range(count):
                now = e + (jj - j) * count + b
                if e + b >= first:
                    partner_copy(now, 1).wait_recv()
                elif e + b + (steps - 1) * count >= first:
                    @pl.when(now >= first)
                    def _():
                        partner_copy(now, 1).wait_recv()
                finish_h(now, sums, now - base)

        loop(j, j + steps, before=before, after=send)
        e += count * steps
        j += steps
        for group in range(n_staged):
            if stage_of[group] is not None and stage_of[group][0] < 1 and j - stage_of[group][1] >= 3:
                next_stage(group, 1)
                stage_of[group] = (1, j)
        for group, end in enumerate(ends):
            if e == end:
                send_stage(group, 0)
                stage_of[group] = (0, j)

    while e < n - 1:
        partner_copy(e, 1).wait_recv()
        sums, base = place(e)
        finish_h(e, sums, e - base)
        e += 1
    a_copy(2 * n - 1).wait()
    ybuf[rows_of(n - 1), :] = product(2 * n - 1)
    partner_copy(n - 1, 1).wait_recv()
    finish_h(n - 1, last_sq, n - 1 - ends[-1])
    send_last()

    for stage in range(1, len(STAGES)):
        for group in range(n_staged):
            if stage > stage_of[group][0]:
                next_stage(group, stage)
    for group, end in enumerate(ends):
        finish_n(end - STAGED[group], staged_sums(group))
    partner_copy(0, first).wait_send()
    for j in range(first, n):
        partner_copy(j, 1).wait_send()
    for group in range(n_staged):
        for stage in range(len(STAGES)):
            wait_stage(group, stage, ssend_sem)
    wait_last(qsend_sem)
    wait_last(qrecv_sem)
    finish_n(ends[-1], jnp.sum(last_parts[...], axis=0))


def write_kernel(h, n, h_out, n_out, sem):
    copies = []
    rows = h.shape[0] // OUT_PARTS
    for i, (src, dst) in enumerate(((h, h_out), (n, n_out))):
        for k in range(OUT_PARTS):
            part = pl.ds(k * rows, rows)
            copies.append(pltpu.make_async_copy(src.at[part], dst.at[part], sem.at[i, k]))
    for copy in copies:
        copy.start()
    for copy in copies:
        copy.wait()


def solution(mesh):
    def local_step(attn_blk, w_blk, res_blk, gain_blk):
        rows, cols = res_blk.shape
        n = rows // T
        per = T // 128
        last = (n - sum(STAGED)) * per
        hbm = pl.BlockSpec(memory_space=pltpu.HBM)
        vmem = pl.BlockSpec(memory_space=pltpu.VMEM)
        out = jax.ShapeDtypeStruct((rows, cols), BF16)
        h, normed = pl.pallas_call(
            kernel,
            out_shape=(out, out),
            in_specs=[hbm] * 4,
            out_specs=(vmem, vmem),
            scratch_shapes=[
                pltpu.VMEM((NB, T, attn_blk.shape[1]), BF16),
                pltpu.VMEM(w_blk.shape, BF16),
                pltpu.VMEM((rows, cols), BF16),
                pltpu.VMEM((1, cols), F32),
                pltpu.VMEM((rows, cols), BF16),
                pltpu.VMEM((rows, cols), BF16),
                pltpu.VMEM((rows, cols), BF16),
                pltpu.VMEM((rows, cols), F32),
                pltpu.VMEM((last, 128), F32),
                pltpu.VMEM((PEERS + 1, last, 128), F32),
                *(pltpu.VMEM((len(STAGES), c * per, 128), F32) for c in STAGED),
                *(pltpu.VMEM((len(STAGES), SIDE, c * per, 128), F32) for c in STAGED),
                pltpu.SemaphoreType.DMA((NB,)),
                pltpu.SemaphoreType.DMA,
                pltpu.SemaphoreType.DMA,
                pltpu.SemaphoreType.DMA,
                pltpu.SemaphoreType.DMA((n,)),
                pltpu.SemaphoreType.DMA((n,)),
                pltpu.SemaphoreType.DMA,
                pltpu.SemaphoreType.DMA,
                pltpu.SemaphoreType.DMA((len(STAGED), len(STAGES))),
                pltpu.SemaphoreType.DMA((len(STAGED), len(STAGES))),
            ],
            compiler_params=pltpu.CompilerParams(collective_id=0, has_side_effects=True, vmem_limit_bytes=40 * 2**20),
        )(*(pltpu.with_memory_space_constraint(v, pltpu.HBM) for v in (attn_blk, w_blk, res_blk, gain_blk.reshape(1, cols))))
        return pl.pallas_call(
            write_kernel,
            out_shape=(out, out),
            in_specs=[vmem] * 2,
            out_specs=(hbm, hbm),
            scratch_shapes=[pltpu.SemaphoreType.DMA((2, OUT_PARTS))],
            compiler_params=pltpu.CompilerParams(vmem_limit_bytes=16 * 2**20),
        )(h, normed)

    row_spec = P(("dp", "tp"), "tp2")
    return jax.shard_map(
        local_step, mesh=mesh, in_specs=(P("dp", "tp"), P("tp", "tp2"), row_spec, P("tp2")),
        out_specs=(row_spec, row_spec), check_vma=False,
    )
```

time: 41 us -> 40.1 us (0.978)
  local copies, waits for them, and re-layouts: 1.94 us -> 0 us
  Pallas kernels: 38.3 us -> 39.4 us
    unnamed x2 -> x0, local copies, waits for them, and re-layouts: 1.94 us -> none
    pallas_call x0 -> x1, Pallas kernels: none -> 1.35 us  [local_step(): pl.pallas_call(write_kernel, out_shape=(out, out), in_specs=[vmem] * 2, o...]
where the time goes in v2:
time: 40.1 us; the launch traced here: 40 us
  Pallas kernels  39.4 us (98%)
  between operations  0.64 us (2%)
    pallas_call x1, Pallas kernels, local_step(): pl.pallas_call(kernel, out_shape=(out, out), in_specs=[hbm] * 4, out_spec...  38 us
    pallas_call x1, Pallas kernels, local_step(): pl.pallas_call(write_kernel, out_shape=(out, out), in_specs=[vmem] * 2, o...  1.35 us

profile of v2, /device:TPU:0, one launch (start us, length us, event | category | flops | bytes accessed | tf_op | source)
XLA Modules:
  0.0 40.0 jit_solution(2718006327177669964)
XLA Ops:
  0.6 38.0 %shard_map.59 = (bf16[4096,128]{1,0:T(8,128)(2,1)S(1)}, bf16[4096,128]{1,0:T(8,128)(2,1)S(1)}) custom-call(bf16[8192,4096]{1,0:T(8,128)(2,1)} %a.1, bf16[4096,128]{1,0:T(8,128)(2,1)} %w.1, bf16[4096,128]{1,0:T(8,128)(2,1)} %res.1, f32[1,128]{1,0:T(1,128)} %bitcast.1), custom_call_target="tpu_custom_call" | custom-call | tf_op jit(solution)/shard_map/pallas_call | solution.py:292
  38.6 1.3 %shard_map.60 = (bf16[4096,128]{1,0:T(8,128)(2,1)}, bf16[4096,128]{1,0:T(8,128)(2,1)}) custom-call(bf16[4096,128]{1,0:T(8,128)(2,1)S(1)} %get-tuple-element.4.h, bf16[4096,128]{1,0:T(8,128)(2,1)S(1)} %get-tuple-element.5.n), custom_call_target="tpu_custom_call" | custom-call | tf_op jit(solution)/shard_map/pallas_call | solution.py:323

commit v3 on v2

--- a/solution.py
+++ b/solution.py
@@ -17,7 +17,7 @@
 HEAD = 2
 BARRIER_AT = 4
 EPI_FROM = 7
-STAGED = (8, 5)
+STAGED = ((8, ((2,), (1,), (0,))), (5, ((1, 2), (0,))))
 SIDE = 4
 OUT_PARTS = 2
 
@@ -31,7 +31,10 @@
     key=lambda o: -sum(map(ring_distance, o)),
 )
 PEERS = len(OFFSETS)
-STAGES = tuple(tuple(tuple(d if i == axis else 0 for i in range(3)) for d in (2, 1, 3)) for axis in (2, 1, 0))
+
+
+def stage_offsets(axes):
+    return [o for o in OFFSETS if all(o[i] == 0 for i in range(3) if i not in axes)]
 
 
 def kernel(a, w, res, gain, h_out, n_out, abuf, wbuf, rbuf, gbuf, sendbuf, recvbuf, ybuf, hbuf, last_sq, last_parts, *rest):
@@ -101,27 +104,34 @@
             sums[pl.ds(at * per + b, 1), :] = jnp.sum(block, axis=0, keepdims=True)
 
     def send_stage(group, stage):
+        axes = STAGED[group][1][stage]
+        here = 0
+        for axis in axes:
+            here = here * SIDE + (z, y, x)[axis]
         parts = staged_parts[group]
-        here = (x, y, z)[stage]
-        parts[stage, here] = staged_sq[group][stage]
-        for o in STAGES[stage]:
+        for o in stage_offsets(axes):
             pltpu.make_async_remote_copy(
                 src_ref=staged_sq[group].at[stage], dst_ref=parts.at[stage, here], send_sem=ssend_sem.at[group, stage],
                 recv_sem=srecv_sem.at[group, stage], device_id=peer(o), device_id_type=MESH,
             ).start()
+        parts[stage, here] = staged_sq[group][stage]
 
     def wait_stage(group, stage, sem):
-        whole = staged_parts[group].at[stage, pl.ds(0, SIDE - 1)]
+        whole = staged_parts[group].at[stage, pl.ds(0, SIDE ** len(STAGED[group][1][stage]) - 1)]
         pltpu.make_async_copy(whole, whole, sem.at[group, stage]).wait()
+
+    def stage_sums(group, stage):
+        return jnp.sum(staged_parts[group][stage, 0:SIDE ** len(STAGED[group][1][stage])], axis=0)
 
     def next_stage(group, stage):
         wait_stage(group, stage - 1, srecv_sem)
-        staged_sq[group][stage] = jnp.sum(staged_parts[group][stage - 1], axis=0)
+        staged_sq[group][stage] = stage_sums(group, stage - 1)
         send_stage(group, stage)
 
     def staged_sums(group):
-        wait_stage(group, len(STAGES) - 1, srecv_sem)
-        return jnp.sum(staged_parts[group][len(STAGES) - 1], axis=0)
+        stage = len(STAGED[group][1]) - 1
+        wait_stage(group, stage, srecv_sem)
+        return stage_sums(group, stage)
 
     def send_last():
         for o in OFFSETS:
@@ -190,18 +200,13 @@
     r_copy.wait()
     g_copy.wait()
 
-    ends = [sum(STAGED[:i + 1]) for i in range(n_staged)]
+    ends = [sum(c for c, _ in STAGED[:i + 1]) for i in range(n_staged)]
 
     def place(e):
         for group, end in enumerate(ends):
             if e < end:
-                return staged_sq[group].at[0], end - STAGED[group]
+                return staged_sq[group].at[0], end - STAGED[group][0]
         return last_sq, ends[-1]
-
-    def events(done):
-        for group, end in enumerate(ends):
-            if done == end:
-                send_stage(group, 0)
 
     e, j = 0, EPI_FROM
     stage_of = [None] * n_staged
@@ -250,17 +255,17 @@
     finish_h(n - 1, last_sq, n - 1 - ends[-1])
     send_last()
 
-    for stage in range(1, len(STAGES)):
-        for group in range(n_staged):
-            if stage > stage_of[group][0]:
+    for stage in range(1, max(len(stages) for _, stages in STAGED)):
+        for group, (_, stages) in enumerate(STAGED):
+            if stage_of[group][0] < stage < len(stages):
                 next_stage(group, stage)
     for group, end in enumerate(ends):
-        finish_n(end - STAGED[group], staged_sums(group))
+        finish_n(end - STAGED[group][0], staged_sums(group))
     partner_copy(0, first).wait_send()
     for j in range(first, n):
         partner_copy(j, 1).wait_send()
     for group in range(n_staged):
-        for stage in range(len(STAGES)):
+        for stage in range(len(STAGED[group][1])):
             wait_stage(group, stage, ssend_sem)
     wait_last(qsend_sem)
     wait_last(qrecv_sem)
@@ -285,7 +290,8 @@
         rows, cols = res_blk.shape
         n = rows // T
         per = T // 128
-        last = (n - sum(STAGED)) * per
+        last = (n - sum(c for c, _ in STAGED)) * per
+        n_stages = max(len(stages) for _, stages in STAGED)
         hbm = pl.BlockSpec(memory_space=pltpu.HBM)
         vmem = pl.BlockSpec(memory_space=pltpu.VMEM)
         out = jax.ShapeDtypeStruct((rows, cols), BF16)
@@ -305,8 +311,11 @@
                 pltpu.VMEM((rows, cols), F32),
                 pltpu.VMEM((last, 128), F32),
                 pltpu.VMEM((PEERS + 1, last, 128), F32),
-                *(pltpu.VMEM((len(STAGES), c * per, 128), F32) for c in STAGED),
-                *(pltpu.VMEM((len(STAGES), SIDE, c * per, 128), F32) for c in STAGED),
+                *(pltpu.VMEM((len(stages), c * per, 128), F32) for c, stages in STAGED),
+                *(
+                    pltpu.VMEM((len(stages), SIDE ** max(len(axes) for axes in stages), c * per, 128), F32)
+                    for c, stages in STAGED
+                ),
                 pltpu.SemaphoreType.DMA((NB,)),
                 pltpu.SemaphoreType.DMA,
                 pltpu.SemaphoreType.DMA,
@@ -315,8 +324,8 @@
                 pltpu.SemaphoreType.DMA((n,)),
                 pltpu.SemaphoreType.DMA,
                 pltpu.SemaphoreType.DMA,
-                pltpu.SemaphoreType.DMA((len(STAGED), len(STAGES))),
-                pltpu.SemaphoreType.DMA((len(STAGED), len(STAGES))),
+                pltpu.SemaphoreType.DMA((len(STAGED), n_stages)),
+                pltpu.SemaphoreType.DMA((len(STAGED), n_stages)),
             ],
             compiler_params=pltpu.CompilerParams(collective_id=0, has_side_effects=True, vmem_limit_bytes=40 * 2**20),
         )(*(pltpu.with_memory_space_constraint(v, pltpu.HBM) for v in (attn_blk, w_blk, res_blk, gain_blk.reshape(1, cols))))

time: 40.1 us -> 38.4 us (0.958)
  Pallas kernels: 39.4 us -> 37.6 us
    pallas_call x1, Pallas kernels: 38 us -> 36.3 us  [local_step(): pl.pallas_call(kernel, out_shape=(out, out), in_specs=[hbm] * 4, out_spec...]
where the time goes in v3:
time: 38.4 us; the launch traced here: 38.3 us
  Pallas kernels  37.6 us (98%)
  between operations  0.64 us (2%)
    pallas_call x1, Pallas kernels, local_step(): pl.pallas_call(kernel, out_shape=(out, out), in_specs=[hbm] * 4, out_spec...  36.3 us
    pallas_call x1, Pallas kernels, local_step(): pl.pallas_call(write_kernel, out_shape=(out, out), in_specs=[vmem] * 2, o...  1.35 us

profile of v3, /device:TPU:0, one launch (start us, length us, event | category | flops | bytes accessed | tf_op | source)
XLA Modules:
  0.0 38.3 jit_solution(666783656741296985)
XLA Ops:
  0.6 36.3 %shard_map.59 = (bf16[4096,128]{1,0:T(8,128)(2,1)S(1)}, bf16[4096,128]{1,0:T(8,128)(2,1)S(1)}) custom-call(bf16[8192,4096]{1,0:T(8,128)(2,1)} %a.1, bf16[4096,128]{1,0:T(8,128)(2,1)} %w.1, bf16[4096,128]{1,0:T(8,128)(2,1)} %res.1, f32[1,128]{1,0:T(1,128)} %bitcast.1), custom_call_target="tpu_custom_call" | custom-call | tf_op jit(solution)/shard_map/pallas_call | solution.py:298
  36.9 1.3 %shard_map.60 = (bf16[4096,128]{1,0:T(8,128)(2,1)}, bf16[4096,128]{1,0:T(8,128)(2,1)}) custom-call(bf16[4096,128]{1,0:T(8,128)(2,1)S(1)} %get-tuple-element.4.h, bf16[4096,128]{1,0:T(8,128)(2,1)S(1)} %get-tuple-element.5.n), custom_call_target="tpu_custom_call" | custom-call | tf_op jit(solution)/shard_map/pallas_call | solution.py:332

commit v4 on v3

--- a/solution.py
+++ b/solution.py
@@ -17,7 +17,8 @@
 HEAD = 2
 BARRIER_AT = 4
 EPI_FROM = 7
-STAGED = ((8, ((2,), (1,), (0,))), (5, ((1, 2), (0,))))
+STAGED = ((8, ((1, 2), (0,))), (5, ((1, 2), (0,))))
+STAGE_STEPS = 4
 SIDE = 4
 OUT_PARTS = 2
 
@@ -56,12 +57,17 @@
 
     def chunk_row(q):
         if isinstance(q, int):
-            mine, j = (False, 0) if q == 0 else (True, n - 1) if q == 2 * n - 1 else (q % 2 == 0, (q - 1) // 2 + (q % 2))
+            if q >= 2 * n - 3:
+                mine, j = True, q - n
+            elif q == 2 * n - 4:
+                mine, j = False, n - 1
+            else:
+                mine, j = q % 2 == 0 and q > 0, q // 2 + q % 2 - (1 if q % 2 == 0 and q > 0 else 0)
             half = core if mine else 1 - core
         else:
-            first, last, even = q == 0, q == 2 * n - 1, q % 2 == 0
-            mine = jnp.logical_and(jnp.logical_or(even, last), jnp.logical_not(first))
-            j = jnp.where(first, 0, jnp.where(last, n - 1, (q - 1) // 2 + q % 2))
+            end, swap, even = q >= 2 * n - 3, q == 2 * n - 4, q % 2 == 0
+            mine = jnp.logical_or(end, jnp.logical_and(even, jnp.logical_not(swap)))
+            j = jnp.where(end, q - n, jnp.where(swap, n - 1, (q - 1) // 2 + q % 2))
             half = jnp.where(mine, core, 1 - core)
         return pl.multiple_of(half * own_rows + j * T, T)
 
@@ -165,15 +171,18 @@
     def product(q):
         return jnp.dot(abuf[q % NB], wbuf[...], preferred_element_type=F32).astype(BF16)
 
+    def step(j, before, *places):
+        request(2 * j + AHEAD + 1)
+        request(2 * j + AHEAD + 2)
+        a_copy(2 * j + 1).wait()
+        a_copy(2 * j + 2).wait()
+        before(j)
+        for i, (buffer, chunk) in enumerate(places):
+            buffer[rows_of(chunk), :] = product(2 * j + 1 + i)
+
     def loop(low, high, before=lambda j: None, after=lambda j: None):
         def body(j, _):
-            request(2 * j + AHEAD + 1)
-            request(2 * j + AHEAD + 2)
-            a_copy(2 * j + 1).wait()
-            a_copy(2 * j + 2).wait()
-            before(j)
-            sendbuf[rows_of(j + 1), :] = product(2 * j + 1)
-            ybuf[rows_of(j), :] = product(2 * j + 2)
+            step(j, before, (sendbuf, j + 1), (ybuf, j))
             after(j)
             return 0
 
@@ -210,12 +219,22 @@
 
     e, j = 0, EPI_FROM
     stage_of = [None] * n_staged
-    while j < n - 1:
+
+    def exchange():
+        for group, end in enumerate(ends):
+            if stage_of[group] is not None and stage_of[group][0] < 1 and j - stage_of[group][1] >= STAGE_STEPS:
+                next_stage(group, 1)
+                stage_of[group] = (1, j)
+            if stage_of[group] is None and e == end:
+                send_stage(group, 0)
+                stage_of[group] = (0, j)
+
+    while j < n - 3:
         count = 2 if e + 2 <= j else 1
         sums, base = place(e)
         steps = 1
         while (
-            j + steps < n - 1 and (2 if e + count * steps + 2 <= j + steps else 1) == count
+            j + steps < n - 3 and (2 if e + count * steps + 2 <= j + steps else 1) == count
             and place(e + count * steps)[1] == base and e + count * steps not in ends
             and (e >= first) == (e + count * steps >= first)
         ):
@@ -235,24 +254,27 @@
         loop(j, j + steps, before=before, after=send)
         e += count * steps
         j += steps
-        for group in range(n_staged):
-            if stage_of[group] is not None and stage_of[group][0] < 1 and j - stage_of[group][1] >= 3:
-                next_stage(group, 1)
-                stage_of[group] = (1, j)
-        for group, end in enumerate(ends):
-            if e == end:
-                send_stage(group, 0)
-                stage_of[group] = (0, j)
-
-    while e < n - 1:
-        partner_copy(e, 1).wait_recv()
-        sums, base = place(e)
-        finish_h(e, sums, e - base)
-        e += 1
+        exchange()
+
+    def finish_one(now):
+        partner_copy(now, 1).wait_recv()
+        sums, base = place(now)
+        finish_h(now, sums, now - base)
+
+    ready = e
+    step(n - 3, lambda _: [finish_one(i) for i in range(ready, n - 3)], (sendbuf, n - 2), (sendbuf, n - 1))
+    send(n - 3)
+    send(n - 2)
+    e, j = n - 3, n - 2
+    exchange()
+    step(n - 2, lambda _: None, (ybuf, n - 3), (ybuf, n - 2))
+    j = n - 1
+    exchange()
     a_copy(2 * n - 1).wait()
+    finish_one(n - 3)
+    finish_one(n - 2)
     ybuf[rows_of(n - 1), :] = product(2 * n - 1)
-    partner_copy(n - 1, 1).wait_recv()
-    finish_h(n - 1, last_sq, n - 1 - ends[-1])
+    finish_one(n - 1)
     send_last()
 
     for stage in range(1, max(len(stages) for _, stages in STAGED)):

time: 38.4 us -> 37.8 us (0.984)
  Pallas kernels: 37.6 us -> 37.1 us
    pallas_call x1, Pallas kernels: 36.3 us -> 35.7 us  [local_step(): pl.pallas_call(kernel, out_shape=(out, out), in_specs=[hbm] * 4, out_spec...]
where the time goes in v4:
time: 37.8 us; the launch traced here: 37.7 us
  Pallas kernels  37.1 us (98%)
  between operations  0.64 us (2%)
    pallas_call x1, Pallas kernels, local_step(): pl.pallas_call(kernel, out_shape=(out, out), in_specs=[hbm] * 4, out_spec...  35.7 us
    pallas_call x1, Pallas kernels, local_step(): pl.pallas_call(write_kernel, out_shape=(out, out), in_specs=[vmem] * 2, o...  1.35 us

profile of v4, /device:TPU:0, one launch (start us, length us, event | category | flops | bytes accessed | tf_op | source)
XLA Modules:
  0.0 37.7 jit_solution(5932897419002401638)
XLA Ops:
  0.6 35.7 %shard_map.59 = (bf16[4096,128]{1,0:T(8,128)(2,1)S(1)}, bf16[4096,128]{1,0:T(8,128)(2,1)S(1)}) custom-call(bf16[8192,4096]{1,0:T(8,128)(2,1)} %a.1, bf16[4096,128]{1,0:T(8,128)(2,1)} %w.1, bf16[4096,128]{1,0:T(8,128)(2,1)} %res.1, f32[1,128]{1,0:T(1,128)} %bitcast.1), custom_call_target="tpu_custom_call" | custom-call | tf_op jit(solution)/shard_map/pallas_call | solution.py:320
  36.4 1.3 %shard_map.60 = (bf16[4096,128]{1,0:T(8,128)(2,1)}, bf16[4096,128]{1,0:T(8,128)(2,1)}) custom-call(bf16[4096,128]{1,0:T(8,128)(2,1)S(1)} %get-tuple-element.4.h, bf16[4096,128]{1,0:T(8,128)(2,1)S(1)} %get-tuple-element.5.n), custom_call_target="tpu_custom_call" | custom-call | tf_op jit(solution)/shard_map/pallas_call | solution.py:354

commit v5 on v4

--- a/solution.py
+++ b/solution.py
@@ -20,7 +20,6 @@
 STAGED = ((8, ((1, 2), (0,))), (5, ((1, 2), (0,))))
 STAGE_STEPS = 4
 SIDE = 4
-OUT_PARTS = 2
 
 
 def ring_distance(d):
@@ -38,10 +37,18 @@
     return [o for o in OFFSETS if all(o[i] == 0 for i in range(3) if i not in axes)]
 
 
-def kernel(a, w, res, gain, h_out, n_out, abuf, wbuf, rbuf, gbuf, sendbuf, recvbuf, ybuf, hbuf, last_sq, last_parts, *rest):
+def normalize(mean, g, h, out, h_first, out_first):
+    inv = lax.rsqrt(mean + EPS_NORM)
+    for i in range(mean.shape[0]):
+        scale = jnp.transpose(jnp.broadcast_to(inv[i:i + 1, :], (128, 128)))
+        out[pl.ds(out_first + i * 128, 128), :] = (h[pl.ds(h_first + i * 128, 128), :] * scale * g).astype(BF16)
+
+
+def kernel(a, w, res, gain, h_out, n_out, h_last, sums_out, gbuf, abuf, wbuf, rbuf, sendbuf, recvbuf, ybuf, hbuf, last_sq, last_parts, *rest):
     n_staged = len(STAGED)
     staged_sq, staged_parts, rest = rest[:n_staged], rest[n_staged:2 * n_staged], rest[2 * n_staged:]
     a_sem, w_sem, r_sem, g_sem, psend_sem, precv_sem, qsend_sem, qrecv_sem, ssend_sem, srecv_sem = rest
+    ends = [sum(c for c, _ in STAGED[:i + 1]) for i in range(n_staged)]
     core = lax.axis_index("tp")
     me = lax.axis_index("tp2")
     z, y, x = me // (SIDE * SIDE), (me // SIDE) % SIDE, me % SIDE
@@ -102,7 +109,10 @@
         rows = rows_of(e)
         total = ybuf[rows, :].astype(F32) + recvbuf[rows, :].astype(F32)
         h = rbuf[rows, :].astype(F32) + total
-        hbuf[rows, :] = h
+        if isinstance(e, int) and e >= ends[-1]:
+            h_last[(e - ends[-1]) * T:(e - ends[-1] + 1) * T, :] = h
+        else:
+            hbuf[rows, :] = h
         h_out[rows, :] = h.astype(BF16)
         squares = h * h
         for b in range(per):
@@ -152,12 +162,7 @@
         pltpu.make_async_copy(whole, whole, sem).wait()
 
     def finish_n(first, sums):
-        inv = lax.rsqrt(sums / width + EPS_NORM)
-        g = gbuf[...]
-        for i in range(sums.shape[0]):
-            rows = pl.ds(first * T + i * 128, 128)
-            scale = jnp.transpose(jnp.broadcast_to(inv[i:i + 1, :], (128, 128)))
-            n_out[rows, :] = (hbuf[rows, :] * scale * g).astype(BF16)
+        normalize(sums / width, gbuf[...], hbuf, n_out, first * T, first * T)
 
     def request(q):
         if isinstance(q, int):
@@ -209,7 +214,6 @@
     r_copy.wait()
     g_copy.wait()
 
-    ends = [sum(c for c, _ in STAGED[:i + 1]) for i in range(n_staged)]
 
     def place(e):
         for group, end in enumerate(ends):
@@ -291,18 +295,20 @@
             wait_stage(group, stage, ssend_sem)
     wait_last(qsend_sem)
     wait_last(qrecv_sem)
-    finish_n(ends[-1], jnp.sum(last_parts[...], axis=0))
-
-
-def write_kernel(h, n, h_out, n_out, sem):
-    copies = []
-    rows = h.shape[0] // OUT_PARTS
-    for i, (src, dst) in enumerate(((h, h_out), (n, n_out))):
-        for k in range(OUT_PARTS):
-            part = pl.ds(k * rows, rows)
-            copies.append(pltpu.make_async_copy(src.at[part], dst.at[part], sem.at[i, k]))
+    sums_out[...] = jnp.sum(last_parts[...], axis=0) / width
+
+
+def write_kernel(h, n, h_last, mean, gain, h_out, n_out, last_n, sem):
+    early = h.shape[0] - h_last.shape[0]
+    copies = [
+        pltpu.make_async_copy(n.at[pl.ds(0, early)], n_out.at[pl.ds(0, early)], sem.at[0]),
+        pltpu.make_async_copy(h, h_out, sem.at[1]),
+    ]
     for copy in copies:
         copy.start()
+    normalize(mean[...], gain[...], h_last, last_n, 0, 0)
+    copies.append(pltpu.make_async_copy(last_n, n_out.at[pl.ds(early, h_last.shape[0])], sem.at[2]))
+    copies[-1].start()
     for copy in copies:
         copy.wait()
 
@@ -317,16 +323,16 @@
         hbm = pl.BlockSpec(memory_space=pltpu.HBM)
         vmem = pl.BlockSpec(memory_space=pltpu.VMEM)
         out = jax.ShapeDtypeStruct((rows, cols), BF16)
-        h, normed = pl.pallas_call(
+        last_rows = jax.ShapeDtypeStruct((last * 128, cols), F32)
+        finished = pl.pallas_call(
             kernel,
-            out_shape=(out, out),
+            out_shape=(out, out, last_rows, jax.ShapeDtypeStruct((last, 128), F32), jax.ShapeDtypeStruct((1, cols), F32)),
             in_specs=[hbm] * 4,
-            out_specs=(vmem, vmem),
+            out_specs=(vmem,) * 5,
             scratch_shapes=[
                 pltpu.VMEM((NB, T, attn_blk.shape[1]), BF16),
                 pltpu.VMEM(w_blk.shape, BF16),
                 pltpu.VMEM((rows, cols), BF16),
-                pltpu.VMEM((1, cols), F32),
                 pltpu.VMEM((rows, cols), BF16),
                 pltpu.VMEM((rows, cols), BF16),
                 pltpu.VMEM((rows, cols), BF16),
@@ -354,11 +360,11 @@
         return pl.pallas_call(
             write_kernel,
             out_shape=(out, out),
-            in_specs=[vmem] * 2,
+            in_specs=[vmem] * 5,
             out_specs=(hbm, hbm),
-            scratch_shapes=[pltpu.SemaphoreType.DMA((2, OUT_PARTS))],
+            scratch_shapes=[pltpu.VMEM((last * 128, cols), BF16), pltpu.SemaphoreType.DMA((3,))],
             compiler_params=pltpu.CompilerParams(vmem_limit_bytes=16 * 2**20),
-        )(h, normed)
+        )(*finished)
 
     row_spec = P(("dp", "tp"), "tp2")
     return jax.shard_map(

time: 37.8 us -> 37.6 us (level)
  no operation moved by 1% of the time
where the time goes in v5:
time: 37.6 us; the launch traced here: 37.5 us
  Pallas kernels  36.9 us (98%)
  between operations  0.64 us (2%)
    pallas_call x1, Pallas kernels, local_step(): pl.pallas_call(kernel, out_shape=(out, out, last_rows, jax.ShapeDtypeStru...  35.6 us
    pallas_call x1, Pallas kernels, local_step(): pl.pallas_call(write_kernel, out_shape=(out, out), in_specs=[vmem] * 5, o...  1.33 us

profile of v5, /device:TPU:0, one launch (start us, length us, event | category | flops | bytes accessed | tf_op | source)
XLA Modules:
  0.0 37.5 jit_solution(8450135217176901827)
XLA Ops:
  0.6 35.6 %shard_map.59 = (bf16[4096,128]{1,0:T(8,128)(2,1)S(1)}, bf16[4096,128]{1,0:T(8,128)(2,1)S(1)}, f32[768,128]{1,0:T(8,128)S(1)}, f32[6,128]{1,0:T(8,128)S(1)}, f32[1,128]{1,0:T(1,128)S(1)}) custom-call(bf16[8192,4096]{1,0:T(8,128)(2,1)} %a.1, bf16[4096,128]{1,0:T(8,128)(2,1)} %w.1, bf16[4096,128]{1,0:T(8,128)(2,1)} %res.1, f32[1,128]{1,0:T(1,128)} %bitcast.1), custom_call_target="tpu_custom_call" | custom-call | tf_op jit(solution)/shard_map/pallas_call | solution.py:327
  36.2 1.3 %shard_map.60 = (bf16[4096,128]{1,0:T(8,128)(2,1)}, bf16[4096,128]{1,0:T(8,128)(2,1)}) custom-call(bf16[4096,128]{1,0:T(8,128)(2,1)S(1)} %get-tuple-element.7.h, bf16[4096,128]{1,0:T(8,128)(2,1)S(1)} %get-tuple-element.8.n, f32[768,128]{1,0:T(8,128)S(1)} %get-tuple-element.9.h_last, f32[6,128]{1,0:T(8,128)S(1)} %get-tuple-element.10.mean, ...), custom_call_target="tpu_custom_call" | custom-call | tf_op jit(solution)/shard_map/pallas_call | solution.py:360

commit v6 on v5

--- a/solution.py
+++ b/solution.py
@@ -198,9 +198,9 @@
         request(q)
     a_copy(0).wait()
     sendbuf[rows_of(0), :] = product(0)
+    loop(0, BARRIER_AT + 1)
     r_copy.start()
     g_copy.start()
-    loop(0, BARRIER_AT + 1)
 
     pl.semaphore_wait(barrier, PEERS + 1)
     first = BARRIER_AT + 2

time: 37.6 us -> 37.6 us (level)
  no operation moved by 1% of the time
where the time goes in v6:
time: 37.6 us; the launch traced here: 37.5 us
  Pallas kernels  36.8 us (98%)
  between operations  0.64 us (2%)
    pallas_call x1, Pallas kernels, local_step(): pl.pallas_call(kernel, out_shape=(out, out, last_rows, jax.ShapeDtypeStru...  35.5 us
    pallas_call x1, Pallas kernels, local_step(): pl.pallas_call(write_kernel, out_shape=(out, out), in_specs=[vmem] * 5, o...  1.33 us

profile of v6, /device:TPU:0, one launch (start us, length us, event | category | flops | bytes accessed | tf_op | source)
XLA Modules:
  0.0 37.5 jit_solution(20329432511421760)
XLA Ops:
  0.6 35.5 %shard_map.59 = (bf16[4096,128]{1,0:T(8,128)(2,1)S(1)}, bf16[4096,128]{1,0:T(8,128)(2,1)S(1)}, f32[768,128]{1,0:T(8,128)S(1)}, f32[6,128]{1,0:T(8,128)S(1)}, f32[1,128]{1,0:T(1,128)S(1)}) custom-call(bf16[8192,4096]{1,0:T(8,128)(2,1)} %a.1, bf16[4096,128]{1,0:T(8,128)(2,1)} %w.1, bf16[4096,128]{1,0:T(8,128)(2,1)} %res.1, f32[1,128]{1,0:T(1,128)} %bitcast.1), custom_call_target="tpu_custom_call" | custom-call | tf_op jit(solution)/shard_map/pallas_call | solution.py:327
  36.2 1.3 %shard_map.60 = (bf16[4096,128]{1,0:T(8,128)(2,1)}, bf16[4096,128]{1,0:T(8,128)(2,1)}) custom-call(bf16[4096,128]{1,0:T(8,128)(2,1)S(1)} %get-tuple-element.7.h, bf16[4096,128]{1,0:T(8,128)(2,1)S(1)} %get-tuple-element.8.n, f32[768,128]{1,0:T(8,128)S(1)} %get-tuple-element.9.h_last, f32[6,128]{1,0:T(8,128)S(1)} %get-tuple-element.10.mean, ...), custom_call_target="tpu_custom_call" | custom-call | tf_op jit(solution)/shard_map/pallas_call | solution.py:360
